TPU v7x, 256 devices: a whole 4x4x8 slice. The times are simulated.
256 devices in a mesh: frames: 64 (over z, x, core), mp: 4 (over y).
Axes of the slice: x: 4, y: 4, z: 8, core: 2. Of those that a mesh axis runs over, the one named last changes fastest.
Arguments:
- features: bfloat16 [8192, 512], P('frames'), may hold values from -32 to 32
- logit_weight: bfloat16 [512, 640], replicated, may hold values from -1 to 1
- gumbel_perturbation: float32 [8192, 640], P('frames'), may hold values from -3 to 12
- codebook: bfloat16 [640, 384], replicated, may hold values from -6 to 6
- project_weight: bfloat16 [768, 768], P(None, 'mp'), may hold values from -0.21875 to 0.21875
- context: bfloat16 [8192, 768], P('frames', 'mp'), may hold values from -6 to 6
- distractors: int32 [8192, 100], P('frames'), may hold values from 0 to 8191, as said below
- masked: int32 [8192], P('frames'), may hold values from 0 to 1
Outputs:
- scores: float32 [8192, 101], P('frames')
- loss: float32 [], replicated
- diversity: float32 [], replicated
Inputs may be any that keep to these rules, and one draw needn't show every extreme that they name: `distractors`: the distractor of a frame in shard s (frames s * 128 to s * 128 + 127) lies in shard s + o modulo 8192 // 128, with 1 <= |o| <= 3.
All inputs are finite; a program needn't handle non-finite values.
Results may differ from a plain program's by a relative error of at most 0.0049.
Values may be sent and summed in bfloat16 or wider, within the bound.
No kernel may reach another device: no remote copies, remote signals or barrier semaphores. Data moves between devices by JAX's collectives and lax.ppermute only.
A program may use at most 64 MiB of HBM per device.

v0:
```python
import functools

import jax
import jax.numpy as jnp
from jax import lax
from jax.experimental import pallas as pl
from jax.experimental.pallas import tpu as pltpu
from jax.sharding import PartitionSpec as P


V = 320
G = 2
NEG = 100
GUMBEL_SOFTNESS = 2.0
LOGIT_SOFTNESS = 0.1
NORM_EPSILON = 1e-06

F32 = jnp.float32
BF16 = jnp.bfloat16
I32 = jnp.int32

BLOCKS = 6

SELF_ROW = 100
CTX_ROW = 101
OWN_NORM_ROW = 102
NORM_ROW = 104
PAYLOAD_ROWS = 112

PROB_ROWS = 16
CLASSES = 8
CUT = 16
LOSS_LANE = 80

VMEM = pltpu.MemorySpace.VMEM
HBM = pltpu.MemorySpace.HBM
PARAMS = pltpu.CompilerParams(vmem_limit_bytes=8 << 20)


def group_stats(values, first, reduce, empty):
    head = values[:, : V - V % 128]
    middle = values[:, V - V % 128 : V - V % 128 + 128]
    tail = values[:, V - V % 128 + 128 :]
    low = reduce(
        jnp.concatenate([head, jnp.where(first, middle, empty)], axis=1), axis=1, keepdims=True
    )
    high = reduce(
        jnp.concatenate([jnp.where(first, empty, middle), tail], axis=1), axis=1, keepdims=True
    )
    return low, high


def by_group(low, high, first):
    count = first.shape[0]
    return jnp.concatenate(
        [
            jnp.broadcast_to(low, (count, V - V % 128)),
            jnp.where(first, low, high),
            jnp.broadcast_to(high, (count, V - V % 128)),
        ],
        axis=1,
    )


def group_softmax(values, first):
    shift = by_group(*group_stats(values, first, jnp.max, -jnp.inf), first)
    powers = jnp.exp(values - shift)
    low, high = group_stats(powers, first, jnp.sum, 0.0)
    return powers * by_group(1.0 / low, 1.0 / high, first)


def bf16_parts(values):
    high = values.astype(BF16).astype(F32)
    middle = (values - high).astype(BF16).astype(F32)
    return high, middle, values - high - middle


def target_kernel(feat_hbm, lw_hbm, gum_hbm, cb_hbm, wt_hbm, tgt_ref, feat, lw, gum, cb, wt, sems):
    copies = [
        pltpu.make_async_copy(src, dst, sems.at[i])
        for i, (src, dst) in enumerate(
            ((feat_hbm, feat), (lw_hbm, lw), (gum_hbm, gum), (cb_hbm, cb), (wt_hbm, wt))
        )
    ]
    for copy in copies:
        copy.start()
    copies[0].wait()
    copies[1].wait()
    logits = jnp.dot(feat[...], lw[...], preferred_element_type=F32)
    first = lax.broadcasted_iota(I32, (logits.shape[0], 128), 1) < V % 128
    copies[2].wait()
    soft = group_softmax((logits + gum[...]) / GUMBEL_SOFTNESS, first)
    middle = soft[:, 256:384]
    soft_low = jnp.concatenate([soft[:, :256], jnp.where(first, middle, 0.0)], axis=1)
    soft_high = jnp.concatenate([jnp.where(first, 0.0, middle), soft[:, 384:]], axis=1)
    copies[3].wait()
    codevec = jnp.concatenate(
        [
            jnp.dot(part.astype(BF16), cb[at : at + 384, :], preferred_element_type=F32)
            for part, at in ((soft_low, 0), (soft_high, 256))
        ],
        axis=1,
    ).astype(BF16)
    copies[4].wait()
    target = lax.dot_general(
        wt[...], codevec, (((1,), (1,)), ((), ())), preferred_element_type=F32
    )
    width = target.shape[0]
    tgt_ref[0:width, :] = target.astype(BF16)
    probs = jnp.sum(group_softmax(logits, first), axis=0, keepdims=True)
    tgt_ref[width:, :] = jnp.concatenate(
        [
            part[:, at : at + 128]
            for part in bf16_parts(probs)
            for at in range(0, G * V, 128)
        ]
        + [jnp.zeros((1, 128), F32)],
        axis=0,
    ).astype(BF16)


def prepare_kernel(
    ctxt_hbm, mask_hbm, idxt_hbm, tgt_ref, rows_ref, ctx_ref, code_kt_ref, code_tk_ref,
    ctxt, mask, idxt, sems,
):
    copies = [
        pltpu.make_async_copy(src, dst, sems.at[i])
        for i, (src, dst) in enumerate(
            ((ctxt_hbm, ctxt), (mask_hbm, mask), (idxt_hbm, idxt.at[pl.ds(0, NEG)]))
        )
    ]
    for copy in copies:
        copy.start()
    own = lax.axis_index("frames")
    partner = 1 - 2 * lax.rem(own, 2)
    inner = 2 - 4 * lax.rem(own // 2, 2)
    distances = (partner, inner, -inner, -3 * partner, inner + partner, partner - inner)
    for copy in copies:
        copy.wait()
    wide = tgt_ref[0 : ctxt.shape[0], :].astype(F32)
    context = ctxt[...].astype(F32)
    rows_ref[...] = jnp.zeros_like(rows_ref)
    rows_ref[0:1, :] = jnp.sum(wide * context, axis=0, keepdims=True)
    rows_ref[1:2, :] = jnp.sum(context * context, axis=0, keepdims=True)
    rows_ref[2:3, :] = jnp.sum(wide * wide, axis=0, keepdims=True)
    rows_ref[3:4, :] = mask[...].astype(F32)
    ctx_ref[...] = jnp.transpose(context).astype(BF16)
    row = lax.broadcasted_iota(I32, idxt.shape, 0)
    index = jnp.where(row < NEG, idxt[...], 0)
    offset = (((index >> 7) - own + 32) & 63) - 32
    block = jnp.zeros_like(index)
    for i, o in enumerate(distances):
        block = jnp.where(offset == o, i, block)
    code = (index & 127) + (block << 7)
    code_kt_ref[...] = code
    code_tk_ref[...] = jnp.transpose(code)


def lane_pick(values, index):
    return jnp.take_along_axis(values, index, axis=1, mode="promise_in_bounds")


def pick(picked, block, local, sims, which):
    return jnp.where(block == which, lane_pick(sims, local), picked)


def first_dots_kernel(
    own_ref, a_ref, b_ref, c_ref, ctx_ref, code_ref, picked_ref, norms_ref, probs_ref
):
    ctx = ctx_ref[...]
    width = ctx.shape[1]
    code = code_ref[...]
    local = code & 127
    block = code >> 7
    picked = jnp.zeros(code.shape, F32)
    probs = own_ref[width:, :].astype(F32)
    norms_ref[...] = jnp.zeros_like(norms_ref)
    for i, ref in ((1, a_ref), (2, b_ref), (3, c_ref)):
        target = ref[0:width, :]
        sims = jnp.dot(ctx, target, preferred_element_type=F32)
        picked = pick(picked, block, local, sims, i)
        wide = target.astype(F32)
        norms_ref[i : i + 1, :] = jnp.sum(wide * wide, axis=0, keepdims=True)
        probs = probs + ref[width:, :].astype(F32)
    picked_ref[...] = picked
    probs_ref[...] = probs


def dots_kernel(
    picked_ref, norms_ref, own_probs_ref, swap_ref, ctx_ref, code_ref, rows_ref,
    out_ref, probs_ref,
):
    ctx = ctx_ref[...]
    width = ctx.shape[1]
    code = code_ref[...]
    local = code & 127
    block = code >> 7
    out_ref[SELF_ROW : SELF_ROW + 4, :] = rows_ref[0:4, :]
    out_ref[NORM_ROW:, :] = norms_ref[...]
    tall = width + PROB_ROWS
    picked = picked_ref[...]
    probs = own_probs_ref[...] + swap_ref[3 * tall :, :].astype(F32)
    for i, at in ((4, 0), (5, tall), (0, 2 * tall)):
        target = swap_ref[at : at + width, :]
        sims = jnp.dot(ctx, target, preferred_element_type=F32)
        picked = pick(picked, block, local, sims, i)
        wide = target.astype(F32)
        out_ref[NORM_ROW + i : NORM_ROW + i + 1, :] = jnp.sum(wide * wide, axis=0, keepdims=True)
        probs = probs + swap_ref[at + width : at + tall, :].astype(F32)
    out_ref[0:NEG, :] = jnp.transpose(picked)[0:NEG, :]
    probs_ref[...] = jnp.zeros_like(probs_ref)
    probs_ref[0:5, :] = probs[0:5, :] + (probs[5:10, :] + probs[10:15, :])


def scores_kernel(p0, p1, p2, p3, code_ref, rows_ref, probs_ref, scores_ref, parts_ref):
    total = (p0[...] + p1[...]) + (p2[...] + p3[...])
    scale = lax.rsqrt(total[CTX_ROW : CTX_ROW + 1, :] + NORM_EPSILON) / LOGIT_SOFTNESS
    inverse = lax.rsqrt(total[OWN_NORM_ROW:, :] + NORM_EPSILON)
    own = total[SELF_ROW : SELF_ROW + 1, :] * inverse[0:1, :] * scale
    code = code_ref[0:104, :]
    local = code & 127
    block = code >> 7
    picked = jnp.zeros(code.shape, F32)
    for i in range(BLOCKS):
        at = NORM_ROW - OWN_NORM_ROW + i
        table = jnp.broadcast_to(inverse[at : at + 1, :], code.shape)
        picked = jnp.where(block == i, lane_pick(table, local), picked)
    others = total[0:104, :] * picked * scale
    row = lax.broadcasted_iota(I32, others.shape, 0)
    powers = jnp.where(row < NEG, jnp.exp(jnp.where(row < NEG, others, 0.0)), 0.0)
    summed = jnp.sum(powers, axis=0, keepdims=True) + jnp.exp(own)
    cross = jnp.where(rows_ref[3:4, :] == 1.0, jnp.log(summed) - own, 0.0)
    scores_ref[0:1, :] = own
    scores_ref[1 : NEG + 1, :] = others[0:NEG, :]
    cut = lax.rem(lax.axis_index("frames"), CLASSES)
    rolled = pltpu.roll(probs_ref[...], 128 - CUT * cut, 1)
    row = lax.broadcasted_iota(I32, rolled.shape, 0)
    lane = lax.broadcasted_iota(I32, rolled.shape, 1)
    line = jnp.where((lane >> 4) + row == 0, rolled, 0.0)
    for i in range(1, G * V // 128):
        here = ((lane >> 4) == i) & (row == i)
        line = jnp.where(here, pltpu.roll(rolled, CUT * i, 1), line)
    line = jnp.sum(line, axis=0, keepdims=True)
    lane = lax.broadcasted_iota(I32, line.shape, 1)
    line = jnp.where(
        lane < LOSS_LANE, line,
        jnp.where(lane == LOSS_LANE, jnp.sum(cross, axis=1, keepdims=True), 0.0),
    )
    parts_ref[...] = jnp.broadcast_to(line[None], parts_ref.shape)


def totals_kernel(frames, parts_ref, held_ref, scores_ref, loss_ref, diversity_ref):
    scores_ref[...] = held_ref[...]
    parts = parts_ref[...]
    parts = parts.reshape(parts.shape[0] // CLASSES, CLASSES, 1, 128)
    total = jnp.sum(parts, axis=0) / frames
    cut = lax.broadcasted_iota(I32, total.shape, 0)
    lane = lax.broadcasted_iota(I32, total.shape, 2)
    column = (lane >> 4) * 128 + cut * CUT + (lane & 15)
    counted = lane < LOSS_LANE
    usage = jnp.where(counted, total, 0.0)
    terms = usage * jnp.log(usage + 1e-07)

    def summed(where):
        rows = jnp.sum(jnp.where(where, terms, 0.0), axis=0)
        return jnp.sum(rows, axis=1, keepdims=True)

    perplex = jnp.exp(-summed(column < V)) + jnp.exp(-summed(column >= V))
    diversity_ref[...] = (G * V - perplex) / (G * V)
    loss = jnp.sum(jnp.where(lane == LOSS_LANE, total, 0.0), axis=0)
    loss_ref[...] = jnp.sum(loss, axis=1, keepdims=True)


def struct(shape, kind):
    return jax.ShapeDtypeStruct(shape, kind)


def exchange(value, shards, replicas, source):
    pairs = []
    for s in range(shards):
        for j in range(replicas):
            pairs.append((source(s) % shards * replicas + j, s * replicas + j))
    return lax.ppermute(value, ("frames", "mp"), pairs)


def on_device(
    features, logit_weight, gumbel, codebook, project_weight, context, distractors, masked
):
    count = features.shape[0]
    shards = lax.axis_size("frames")
    replicas = lax.axis_size("mp")
    weight_t = project_weight.T
    context_t = context.T
    width = context_t.shape[0]
    operands = (features, logit_weight, gumbel, codebook, weight_t)
    target = pl.pallas_call(
        target_kernel,
        out_shape=struct((width + PROB_ROWS, count), BF16),
        in_specs=[pl.BlockSpec(memory_space=HBM)] * 5,
        out_specs=pl.BlockSpec(memory_space=VMEM),
        scratch_shapes=[pltpu.VMEM(x.shape, x.dtype) for x in operands]
        + [pltpu.SemaphoreType.DMA((5,))],
        compiler_params=PARAMS,
        name="target",
    )(*[pltpu.with_memory_space_constraint(x, HBM) for x in operands])
    operands = (context_t, masked.reshape(1, count))
    rows, ctx, code_kt, code_tk = pl.pallas_call(
        prepare_kernel,
        out_shape=(
            struct((8, count), F32),
            struct((count, width), BF16),
            struct((128, count), I32),
            struct((count, 128), I32),
        ),
        in_specs=[pl.BlockSpec(memory_space=HBM)] * 3 + [pl.BlockSpec(memory_space=VMEM)],
        out_specs=[pl.BlockSpec(memory_space=VMEM)] * 4,
        scratch_shapes=[pltpu.VMEM(x.shape, x.dtype) for x in operands]
        + [pltpu.VMEM((128, count), I32), pltpu.SemaphoreType.DMA((3,))],
        compiler_params=PARAMS,
        name="prepare",
    )(*[pltpu.with_memory_space_constraint(x, HBM) for x in (*operands, distractors.T)], target)

    def outer(s):
        return s - 2 if s // 2 % 2 == 0 else s + 2

    def across(s):
        return s - 3 if s % 2 == 0 else s + 3

    send = functools.partial(exchange, shards=shards, replicas=replicas)
    b = send(target, source=outer)
    c = send(target, source=across)
    a = send(target, source=lambda s: s ^ 2)
    a, b, c = lax.optimization_barrier((a, b, c))
    swap = send(jnp.concatenate([a, b, target, c[width:]], axis=0), source=lambda s: s ^ 1)
    picked, norms, probs = pl.pallas_call(
        first_dots_kernel,
        out_shape=(
            struct((count, 128), F32),
            struct((PAYLOAD_ROWS - NORM_ROW, count), F32),
            struct((PROB_ROWS, 128), F32),
        ),
        in_specs=[pl.BlockSpec(memory_space=VMEM)] * 6,
        out_specs=[pl.BlockSpec(memory_space=VMEM)] * 3,
        compiler_params=PARAMS,
        name="first_dots",
    )(target, a, b, c, ctx, code_tk)
    payload, probs = pl.pallas_call(
        dots_kernel,
        out_shape=(struct((PAYLOAD_ROWS, count), F32), struct((8, 128), F32)),
        in_specs=[pl.BlockSpec(memory_space=VMEM)] * 7,
        out_specs=[pl.BlockSpec(memory_space=VMEM)] * 2,
        compiler_params=PARAMS,
        name="dots",
    )(picked, norms, probs, swap, ctx, code_tk, rows)
    peers = []
    for step in (2, 3, 1):
        peers.append(lax.ppermute(payload, "mp", [(j ^ step, j) for j in range(replicas)]))
    scores_t, parts = pl.pallas_call(
        scores_kernel,
        out_shape=(struct((NEG + 1, count), F32), struct((shards, 1, 128), F32)),
        in_specs=[pl.BlockSpec(memory_space=VMEM)] * 7,
        out_specs=[pl.BlockSpec(memory_space=VMEM)] * 2,
        compiler_params=PARAMS,
        name="scores",
    )(payload, *peers, code_kt, rows, probs)
    parts = lax.all_to_all(parts, "frames", split_axis=0, concat_axis=0, tiled=True)
    scores_t, loss, diversity = pl.pallas_call(
        functools.partial(totals_kernel, count * shards),
        out_shape=(struct(scores_t.shape, F32), struct((1, 1), F32), struct((1, 1), F32)),
        in_specs=[pl.BlockSpec(memory_space=VMEM)] * 2,
        out_specs=[pl.BlockSpec(memory_space=VMEM)] * 3,
        compiler_params=PARAMS,
        name="totals",
    )(parts, scores_t)
    return scores_t.T, loss.reshape(()), diversity.reshape(())


def solution(mesh):
    return jax.shard_map(
        on_device,
        mesh=mesh,
        in_specs=(
            P("frames", None),
            P(),
            P("frames", None),
            P(),
            P(None, "mp"),
            P("frames", "mp"),
            P("frames", None),
            P("frames"),
        ),
        out_specs=(P("frames", None), P(), P()),
        check_vma=False,
    )
```

profile of v0, /device:TPU:1, one launch (start us, length us, event | category | flops | bytes accessed | tf_op | source)
XLA Modules:
  0.0 45.2 jit_solution(8253379755782758351)
XLA Ops:
  0.6 2.3 %target.1.tgt_ref.own_ref = bf16[208,128]{1,0:T(8,128)(2,1)S(1)} custom-call(bf16[128,512]{1,0:T(8,128)(2,1)} %feat_hbm.1, bf16[512,640]{1,0:T(8,128)(2,1)} %lw_hbm.1, f32[128,640]{1,0:T(8,128)} %gum_hbm.1, bf16[640,384]{1,0:T(8,128)(2,1)} %cb_hbm.1, bf16[192,768]{1,0:T(8,128)(2,1)} %bitcast.7), custom_call_target="tpu_custom_call" | custom-call | tf_op jit(solution)/shard_map/target/pallas_call | solution.py:296
  2.9 2.1 %collective-permute-start = (bf16[208,128]{1,0:T(8,128)(2,1)S(1)}, bf16[208,128]{1,0:T(8,128)(2,1)S(1)}, u32[]{:S(2)}, u32[]{:S(2)}) collective-permute-start(bf16[208,128]{1,0:T(8,128)(2,1)S(1)} %target.1.tgt_ref.own_ref), channel_id=1, source_target_pairs={{8,0},{9,1},{10,2},{11,3},{12,4},{13,5},{14,6},{15,7},{0,8},{1,9},... | collective-permute-start | bytes 159752 | tf_op jit(solution)/shard_map/ppermute | solution.py:283
  5.0 7.1 %collective-permute-start.1 = (bf16[208,128]{1,0:T(8,128)(2,1)S(1)}, bf16[208,128]{1,0:T(8,128)(2,1)S(1)}, u32[]{:S(2)}, u32[]{:S(2)}) collective-permute-start(bf16[208,128]{1,0:T(8,128)(2,1)S(1)} %target.1.tgt_ref.own_ref), channel_id=1, source_target_pairs={{248,0},{249,1},{250,2},{251,3},{252,4},{253,5},{254,6},{255,7},{1... | collective-permute-start | bytes 159752 | tf_op jit(solution)/shard_map/ppermute | solution.py:283
  12.2 0.0 collective-permute-start.2
  12.2 0.0 collective-permute-done.a_ref
  12.2 1.5 %collective-permute-done.1.b_ref = bf16[208,128]{1,0:T(8,128)(2,1)S(1)} collective-permute-done((bf16[208,128]{1,0:T(8,128)(2,1)S(1)}, bf16[208,128]{1,0:T(8,128)(2,1)S(1)}, u32[]{:S(2)}, u32[]{:S(2)}) %collective-permute-start.1) | collective-permute-done | bytes 53280 | tf_op jit(solution)/shard_map/ppermute | solution.py:283
  13.7 3.5 %collective-permute-done.2.c_ref = bf16[208,128]{1,0:T(8,128)(2,1)S(1)} collective-permute-done((bf16[208,128]{1,0:T(8,128)(2,1)S(1)}, bf16[208,128]{1,0:T(8,128)(2,1)S(1)}, u32[]{:S(2)}, u32[]{:S(2)}) %collective-permute-start.2) | collective-permute-done | bytes 53280 | tf_op jit(solution)/shard_map/ppermute | solution.py:283
  17.2 3.4 %collective-permute-start.3 = (bf16[640,128]{1,0:T(8,128)(2,1)S(1)}, bf16[640,128]{1,0:T(8,128)(2,1)S(1)}, u32[]{:S(2)}, u32[]{:S(2)}) collective-permute-start(bf16[640,128]{1,0:T(8,128)(2,1)S(1)} %pad_maximum_fusion), channel_id=1, source_target_pairs={{4,0},{5,1},{6,2},{7,3},{0,4},{1,5},{2,6},{3,7},{12,8},{13,9},{14,... | collective-permute-start | bytes 491528 | tf_op jit(solution)/shard_map/ppermute | solution.py:283
  20.7 1.0 %prepare.1 = (f32[8,128]{1,0:T(8,128)S(1)}, bf16[128,192]{1,0:T(8,128)(2,1)S(1)}, s32[128,128]{1,0:T(8,128)S(1)}, s32[128,128]{1,0:T(8,128)S(1)}) custom-call(bf16[192,128]{1,0:T(8,128)(2,1)} %bitcast.9, s32[1,128]{1,0:T(1,128)} %bitcast.10, s32[100,128]{1,0:T(8,128)} %bitcast.8, bf16[208,128]{1,0:T(8,128)(2,1)S(1)} %target.1.tgt_ref.own_ref), custom_call_target="tpu_custom_call" | custom-call | tf_op jit(solution)/shard_map/prepare/pallas_call | solution.py:307
  21.7 0.3 first_dots.1
  22.0 0.0 collective-permute-done.3.swap_ref
  22.0 0.4 dots.1
  22.4 3.0 %collective-permute-start.4 = (f32[112,128]{1,0:T(8,128)S(1)}, f32[112,128]{1,0:T(8,128)S(1)}, u32[]{:S(2)}, u32[]{:S(2)}) collective-permute-start(f32[112,128]{1,0:T(8,128)S(1)} %get-tuple-element.29.p0), channel_id=1, source_target_pairs={{2,0},{3,1},{0,2},{1,3},{6,4},{7,5},{4,6},{5,7},{10,8},{11,9},{8,1... | collective-permute-start | bytes 172040 | tf_op jit(solution)/shard_map/ppermute | solution.py:357
  25.4 0.8 %collective-permute-start.5 = (f32[112,128]{1,0:T(8,128)S(1)}, f32[112,128]{1,0:T(8,128)S(1)}, u32[]{:S(2)}, u32[]{:S(2)}) collective-permute-start(f32[112,128]{1,0:T(8,128)S(1)} %get-tuple-element.29.p0), channel_id=1, source_target_pairs={{3,0},{2,1},{1,2},{0,3},{7,4},{6,5},{5,6},{4,7},{11,8},{10,9},{9,1... | collective-permute-start | bytes 172040 | tf_op jit(solution)/shard_map/ppermute | solution.py:357
  26.2 0.0 collective-permute-start.6
  26.2 1.3 %collective-permute-done.4.p1 = f32[112,128]{1,0:T(8,128)S(1)} collective-permute-done((f32[112,128]{1,0:T(8,128)S(1)}, f32[112,128]{1,0:T(8,128)S(1)}, u32[]{:S(2)}, u32[]{:S(2)}) %collective-permute-start.4) | collective-permute-done | bytes 57376 | tf_op jit(solution)/shard_map/ppermute | solution.py:357
  27.5 2.2 %collective-permute-done.5.p2 = f32[112,128]{1,0:T(8,128)S(1)} collective-permute-done((f32[112,128]{1,0:T(8,128)S(1)}, f32[112,128]{1,0:T(8,128)S(1)}, u32[]{:S(2)}, u32[]{:S(2)}) %collective-permute-start.5) | collective-permute-done | bytes 57376 | tf_op jit(solution)/shard_map/ppermute | solution.py:357
  29.7 0.0 collective-permute-done.6.p3
  29.7 0.4 scores.1
  30.1 14.4 %all_to_all.5.parts_ref = f32[64,1,128]{2,1,0:T(1,128)S(1)} all-to-all(f32[64,1,128]{2,1,0:T(1,128)S(1)} %get-tuple-element.32), channel_id=1, replica_groups=mesh['frames'=64,'mp'=4] {'frames'}, dimensions={0} | all-to-all | bytes 65536 | tf_op jit(solution)/shard_map/all_to_all | solution.py:366
  44.5 0.7 %totals.1 = (f32[101,128]{1,0:T(8,128)}, f32[1,1]{1,0:T(1,128)}, f32[1,1]{1,0:T(1,128)}) custom-call(f32[64,1,128]{2,1,0:T(1,128)S(1)} %all_to_all.5.parts_ref, f32[101,128]{1,0:T(8,128)S(1)} %get-tuple-element.33.held_ref), custom_call_target="tpu_custom_call" | custom-call | tf_op jit(solution)/shard_map/totals/pallas_call | solution.py:367
  (2 shorter events, 0.0 us)
Async XLA Ops:
  2.9 9.2 %collective-permute-start = (bf16[208,128]{1,0:T(8,128)(2,1)S(1)}, bf16[208,128]{1,0:T(8,128)(2,1)S(1)}, u32[]{:S(2)}, u32[]{:S(2)}) collective-permute-start(bf16[208,128]{1,0:T(8,128)(2,1)S(1)} %target.1.tgt_ref.own_ref), channel_id=1, source_target_pairs={{8,0},{9,1},{10,2},{11,3},{12,4},{13,5},{14,6},{15,7},{0,8},{1,9},... | collective-permute-start | bytes 159752 | tf_op jit(solution)/shard_map/ppermute | solution.py:283
  5.0 8.6 %collective-permute-start.1 = (bf16[208,128]{1,0:T(8,128)(2,1)S(1)}, bf16[208,128]{1,0:T(8,128)(2,1)S(1)}, u32[]{:S(2)}, u32[]{:S(2)}) collective-permute-start(bf16[208,128]{1,0:T(8,128)(2,1)S(1)} %target.1.tgt_ref.own_ref), channel_id=1, source_target_pairs={{248,0},{249,1},{250,2},{251,3},{252,4},{253,5},{254,6},{255,7},{1... | collective-permute-start | bytes 159752 | tf_op jit(solution)/shard_map/ppermute | solution.py:283
  12.2 5.1 %collective-permute-start.2 = (bf16[208,128]{1,0:T(8,128)(2,1)S(1)}, bf16[208,128]{1,0:T(8,128)(2,1)S(1)}, u32[]{:S(2)}, u32[]{:S(2)}) collective-permute-start(bf16[208,128]{1,0:T(8,128)(2,1)S(1)} %target.1.tgt_ref.own_ref), channel_id=1, source_target_pairs={{244,0},{245,1},{246,2},{247,3},{16,4},{17,5},{18,6},{19,7},{252,8... | collective-permute-start | bytes 159752 | tf_op jit(solution)/shard_map/ppermute | solution.py:283
  17.2 4.8 %collective-permute-start.3 = (bf16[640,128]{1,0:T(8,128)(2,1)S(1)}, bf16[640,128]{1,0:T(8,128)(2,1)S(1)}, u32[]{:S(2)}, u32[]{:S(2)}) collective-permute-start(bf16[640,128]{1,0:T(8,128)(2,1)S(1)} %pad_maximum_fusion), channel_id=1, source_target_pairs={{4,0},{5,1},{6,2},{7,3},{0,4},{1,5},{2,6},{3,7},{12,8},{13,9},{14,... | collective-permute-start | bytes 491528 | tf_op jit(solution)/shard_map/ppermute | solution.py:283
  22.4 5.0 %collective-permute-start.4 = (f32[112,128]{1,0:T(8,128)S(1)}, f32[112,128]{1,0:T(8,128)S(1)}, u32[]{:S(2)}, u32[]{:S(2)}) collective-permute-start(f32[112,128]{1,0:T(8,128)S(1)} %get-tuple-element.29.p0), channel_id=1, source_target_pairs={{2,0},{3,1},{0,2},{1,3},{6,4},{7,5},{4,6},{5,7},{10,8},{11,9},{8,1... | collective-permute-start | bytes 172040 | tf_op jit(solution)/shard_map/ppermute | solution.py:357
  25.4 4.2 %collective-permute-start.5 = (f32[112,128]{1,0:T(8,128)S(1)}, f32[112,128]{1,0:T(8,128)S(1)}, u32[]{:S(2)}, u32[]{:S(2)}) collective-permute-start(f32[112,128]{1,0:T(8,128)S(1)} %get-tuple-element.29.p0), channel_id=1, source_target_pairs={{3,0},{2,1},{1,2},{0,3},{7,4},{6,5},{5,6},{4,7},{11,8},{10,9},{9,1... | collective-permute-start | bytes 172040 | tf_op jit(solution)/shard_map/ppermute | solution.py:357
  26.2 3.5 %collective-permute-start.6 = (f32[112,128]{1,0:T(8,128)S(1)}, f32[112,128]{1,0:T(8,128)S(1)}, u32[]{:S(2)}, u32[]{:S(2)}) collective-permute-start(f32[112,128]{1,0:T(8,128)S(1)} %get-tuple-element.29.p0), channel_id=1, source_target_pairs={{1,0},{0,1},{3,2},{2,3},{5,4},{4,5},{7,6},{6,7},{9,8},{8,9},{11,10... | collective-permute-start | bytes 172040 | tf_op jit(solution)/shard_map/ppermute | solution.py:357
where the time goes:
time: 45.4 us; the launch traced here: 45.2 us
  starting transfers between devices  16.4 us (36%)
  blocking collectives  14.4 us (32%)
  waiting for transfers between devices  8.53 us (19%)
  Pallas kernels  5.09 us (11%)
  between operations  0.68 us (1%)
    all_to_all x1, blocking collectives, on_device(): lax.all_to_all(parts, 'frames', split_axis=0, concat_axis=0, tiled=True)  14.4 us
    ppermute x4, starting transfers between devices, exchange(): return lax.ppermute(value, ('frames', 'mp'), pairs)  12.7 us
    ppermute x4, waiting for transfers between devices, exchange(): return lax.ppermute(value, ('frames', 'mp'), pairs)  5.06 us
    ppermute x3, starting transfers between devices, on_device(): lax.ppermute(payload, 'mp', [(j ^ step, j) for j in range(replicas)])  3.77 us
    ppermute x3, waiting for transfers between devices, on_device(): lax.ppermute(payload, 'mp', [(j ^ step, j) for j in range(replicas)])  3.46 us
    pallas_call x1, Pallas kernels, on_device(): pl.pallas_call(target_kernel, out_shape=struct((width + PROB_ROWS, count)...  2.29 us
    pallas_call x1, Pallas kernels, on_device(): pl.pallas_call(prepare_kernel, out_shape=(struct((8, count), F32), struct...  1.01 us
  transfers between devices with their start and end apart: 7, of which 4 were waited for; matrix products, arithmetic and copies ran while one was open for 0% of the time, Pallas kernels for 3%

commit v1 on v0

--- a/solution.py
+++ b/solution.py
@@ -164,9 +164,7 @@
     return jnp.where(block == which, lane_pick(sims, local), picked)
 
 
-def first_dots_kernel(
-    own_ref, a_ref, b_ref, c_ref, ctx_ref, code_ref, picked_ref, norms_ref, probs_ref
-):
+def first_dots_kernel(own_ref, a_ref, b_ref, ctx_ref, code_ref, picked_ref, norms_ref, probs_ref):
     ctx = ctx_ref[...]
     width = ctx.shape[1]
     code = code_ref[...]
@@ -175,7 +173,7 @@
     picked = jnp.zeros(code.shape, F32)
     probs = own_ref[width:, :].astype(F32)
     norms_ref[...] = jnp.zeros_like(norms_ref)
-    for i, ref in ((1, a_ref), (2, b_ref), (3, c_ref)):
+    for i, ref in ((1, a_ref), (2, b_ref)):
         target = ref[0:width, :]
         sims = jnp.dot(ctx, target, preferred_element_type=F32)
         picked = pick(picked, block, local, sims, i)
@@ -187,8 +185,8 @@
 
 
 def dots_kernel(
-    picked_ref, norms_ref, own_probs_ref, swap_ref, ctx_ref, code_ref, rows_ref,
-    out_ref, probs_ref,
+    picked_ref, norms_ref, own_probs_ref, swap_ref, c_ref, ctx_ref, code_ref, rows_ref,
+    out_ref, probs_ref, edge_ref,
 ):
     ctx = ctx_ref[...]
     width = ctx.shape[1]
@@ -199,20 +197,22 @@
     out_ref[NORM_ROW:, :] = norms_ref[...]
     tall = width + PROB_ROWS
     picked = picked_ref[...]
-    probs = own_probs_ref[...] + swap_ref[3 * tall :, :].astype(F32)
-    for i, at in ((4, 0), (5, tall), (0, 2 * tall)):
-        target = swap_ref[at : at + width, :]
+    edge = c_ref[width:, :].astype(F32)
+    edge_ref[...] = edge
+    probs = own_probs_ref[...] + edge
+    for i, ref, at in ((4, swap_ref, 0), (5, swap_ref, tall), (0, swap_ref, 2 * tall), (3, c_ref, 0)):
+        target = ref[at : at + width, :]
         sims = jnp.dot(ctx, target, preferred_element_type=F32)
         picked = pick(picked, block, local, sims, i)
         wide = target.astype(F32)
         out_ref[NORM_ROW + i : NORM_ROW + i + 1, :] = jnp.sum(wide * wide, axis=0, keepdims=True)
-        probs = probs + swap_ref[at + width : at + tall, :].astype(F32)
+        if i != 3:
+            probs = probs + ref[at + width : at + tall, :].astype(F32)
     out_ref[0:NEG, :] = jnp.transpose(picked)[0:NEG, :]
-    probs_ref[...] = jnp.zeros_like(probs_ref)
-    probs_ref[0:5, :] = probs[0:5, :] + (probs[5:10, :] + probs[10:15, :])
-
-
-def scores_kernel(p0, p1, p2, p3, code_ref, rows_ref, probs_ref, scores_ref, parts_ref):
+    probs_ref[...] = probs
+
+
+def scores_kernel(p0, p1, p2, p3, code_ref, rows_ref, probs_ref, edge_ref, scores_ref, parts_ref):
     total = (p0[...] + p1[...]) + (p2[...] + p3[...])
     scale = lax.rsqrt(total[CTX_ROW : CTX_ROW + 1, :] + NORM_EPSILON) / LOGIT_SOFTNESS
     inverse = lax.rsqrt(total[OWN_NORM_ROW:, :] + NORM_EPSILON)
@@ -233,7 +233,11 @@
     scores_ref[0:1, :] = own
     scores_ref[1 : NEG + 1, :] = others[0:NEG, :]
     cut = lax.rem(lax.axis_index("frames"), CLASSES)
-    rolled = pltpu.roll(probs_ref[...], 128 - CUT * cut, 1)
+    sums = probs_ref[...] + edge_ref[...]
+    sums = jnp.concatenate(
+        [sums[0:5, :] + (sums[5:10, :] + sums[10:15, :]), jnp.zeros((3, 128), F32)], axis=0
+    )
+    rolled = pltpu.roll(sums, 128 - CUT * cut, 1)
     row = lax.broadcasted_iota(I32, rolled.shape, 0)
     lane = lax.broadcasted_iota(I32, rolled.shape, 1)
     line = jnp.where((lane >> 4) + row == 0, rolled, 0.0)
@@ -330,8 +334,7 @@
     b = send(target, source=outer)
     c = send(target, source=across)
     a = send(target, source=lambda s: s ^ 2)
-    a, b, c = lax.optimization_barrier((a, b, c))
-    swap = send(jnp.concatenate([a, b, target, c[width:]], axis=0), source=lambda s: s ^ 1)
+    swap = send(jnp.concatenate([a, b, target], axis=0), source=lambda s: s ^ 1)
     picked, norms, probs = pl.pallas_call(
         first_dots_kernel,
         out_shape=(
@@ -339,30 +342,35 @@
             struct((PAYLOAD_ROWS - NORM_ROW, count), F32),
             struct((PROB_ROWS, 128), F32),
         ),
-        in_specs=[pl.BlockSpec(memory_space=VMEM)] * 6,
+        in_specs=[pl.BlockSpec(memory_space=VMEM)] * 5,
         out_specs=[pl.BlockSpec(memory_space=VMEM)] * 3,
         compiler_params=PARAMS,
         name="first_dots",
-    )(target, a, b, c, ctx, code_tk)
-    payload, probs = pl.pallas_call(
+    )(target, a, b, ctx, code_tk)
+    payload, probs, edge = pl.pallas_call(
         dots_kernel,
-        out_shape=(struct((PAYLOAD_ROWS, count), F32), struct((8, 128), F32)),
-        in_specs=[pl.BlockSpec(memory_space=VMEM)] * 7,
-        out_specs=[pl.BlockSpec(memory_space=VMEM)] * 2,
+        out_shape=(
+            struct((PAYLOAD_ROWS, count), F32),
+            struct((PROB_ROWS, 128), F32),
+            struct((PROB_ROWS, 128), F32),
+        ),
+        in_specs=[pl.BlockSpec(memory_space=VMEM)] * 8,
+        out_specs=[pl.BlockSpec(memory_space=VMEM)] * 3,
         compiler_params=PARAMS,
         name="dots",
-    )(picked, norms, probs, swap, ctx, code_tk, rows)
+    )(picked, norms, probs, swap, c, ctx, code_tk, rows)
+    edge = send(edge, source=lambda s: s ^ 1)
     peers = []
     for step in (2, 3, 1):
         peers.append(lax.ppermute(payload, "mp", [(j ^ step, j) for j in range(replicas)]))
     scores_t, parts = pl.pallas_call(
         scores_kernel,
         out_shape=(struct((NEG + 1, count), F32), struct((shards, 1, 128), F32)),
-        in_specs=[pl.BlockSpec(memory_space=VMEM)] * 7,
+        in_specs=[pl.BlockSpec(memory_space=VMEM)] * 8,
         out_specs=[pl.BlockSpec(memory_space=VMEM)] * 2,
         compiler_params=PARAMS,
         name="scores",
-    )(payload, *peers, code_kt, rows, probs)
+    )(payload, *peers, code_kt, rows, probs, edge)
     parts = lax.all_to_all(parts, "frames", split_axis=0, concat_axis=0, tiled=True)
     scores_t, loss, diversity = pl.pallas_call(
         functools.partial(totals_kernel, count * shards),

time: 45.4 us -> 48.8 us (1.075)
  blocking collectives: 14.4 us -> 17.2 us
  starting transfers between devices: 16.4 us -> 17.7 us
  waiting for transfers between devices: 8.53 us -> 7.96 us
    ppermute x3, waiting for transfers between devices: 3.46 us -> 0.4 us  [on_device(): lax.ppermute(payload, 'mp', [(j ^ step, j) for j in range(replicas)])]
    all_to_all x1, blocking collectives: 14.4 us -> 17.2 us  [on_device(): lax.all_to_all(parts, 'frames', split_axis=0, concat_axis=0, tiled=True)]
    ppermute x4 -> x5, waiting for transfers between devices: 5.06 us -> 7.56 us  [exchange(): return lax.ppermute(value, ('frames', 'mp'), pairs)]
    ppermute x4 -> x5, starting transfers between devices: 12.7 us -> 13.6 us  [exchange(): return lax.ppermute(value, ('frames', 'mp'), pairs)]
  transfers between devices with their start and end apart: 7 -> 8, of which waited for: 4 -> 5; matrix products, arithmetic and copies ran while one was open for 0% -> 0% of each run, Pallas kernels for 3% -> 3%
where the time goes in v1:
time: 48.8 us; the launch traced here: 48.6 us
  starting transfers between devices  17.7 us (36%)
  blocking collectives  17.2 us (35%)
  waiting for transfers between devices  7.96 us (16%)
  Pallas kernels  5.06 us (10%)
  between operations  0.67 us (1%)
    all_to_all x1, blocking collectives, on_device(): lax.all_to_all(parts, 'frames', split_axis=0, concat_axis=0, tiled=True)  17.2 us
    ppermute x5, starting transfers between devices, exchange(): return lax.ppermute(value, ('frames', 'mp'), pairs)  13.6 us
    ppermute x5, waiting for transfers between devices, exchange(): return lax.ppermute(value, ('frames', 'mp'), pairs)  7.56 us
    ppermute x3, starting transfers between devices, on_device(): lax.ppermute(payload, 'mp', [(j ^ step, j) for j in range(replicas)])  4.01 us
    pallas_call x1, Pallas kernels, on_device(): pl.pallas_call(target_kernel, out_shape=struct((width + PROB_ROWS, count)...  2.29 us
    pallas_call x1, Pallas kernels, on_device(): pl.pallas_call(prepare_kernel, out_shape=(struct((8, count), F32), struct...  1.01 us
  transfers between devices with their start and end apart: 8, of which 5 were waited for; matrix products, arithmetic and copies ran while one was open for 0% of the time, Pallas kernels for 3%

profile of v1, /device:TPU:1, one launch (start us, length us, event | category | flops | bytes accessed | tf_op | source)
XLA Modules:
  0.0 48.6 jit_solution(7235888301468755494)
XLA Ops:
  0.6 2.3 %target.1.tgt_ref.own_ref = bf16[208,128]{1,0:T(8,128)(2,1)S(1)} custom-call(bf16[128,512]{1,0:T(8,128)(2,1)} %feat_hbm.1, bf16[512,640]{1,0:T(8,128)(2,1)} %lw_hbm.1, f32[128,640]{1,0:T(8,128)} %gum_hbm.1, bf16[640,384]{1,0:T(8,128)(2,1)} %cb_hbm.1, bf16[192,768]{1,0:T(8,128)(2,1)} %bitcast.7), custom_call_target="tpu_custom_call" | custom-call | tf_op jit(solution)/shard_map/target/pallas_call | solution.py:300
  2.9 8.7 %collective-permute-start.1 = (bf16[208,128]{1,0:T(8,128)(2,1)S(1)}, bf16[208,128]{1,0:T(8,128)(2,1)S(1)}, u32[]{:S(2)}, u32[]{:S(2)}) collective-permute-start(bf16[208,128]{1,0:T(8,128)(2,1)S(1)} %target.1.tgt_ref.own_ref), channel_id=1, source_target_pairs={{248,0},{249,1},{250,2},{251,3},{252,4},{253,5},{254,6},{255,7},{1... | collective-permute-start | bytes 159752 | tf_op jit(solution)/shard_map/ppermute | solution.py:287
  11.6 0.0 collective-permute-start
  11.6 1.5 %collective-permute-done.1.b_ref = bf16[208,128]{1,0:T(8,128)(2,1)S(1)} collective-permute-done((bf16[208,128]{1,0:T(8,128)(2,1)S(1)}, bf16[208,128]{1,0:T(8,128)(2,1)S(1)}, u32[]{:S(2)}, u32[]{:S(2)}) %collective-permute-start.1) | collective-permute-done | bytes 53280 | tf_op jit(solution)/shard_map/ppermute | solution.py:287
  13.1 1.5 %collective-permute-done.a_ref = bf16[208,128]{1,0:T(8,128)(2,1)S(1)} collective-permute-done((bf16[208,128]{1,0:T(8,128)(2,1)S(1)}, bf16[208,128]{1,0:T(8,128)(2,1)S(1)}, u32[]{:S(2)}, u32[]{:S(2)}) %collective-permute-start) | collective-permute-done | bytes 53280 | tf_op jit(solution)/shard_map/ppermute | solution.py:287
  14.6 2.2 %collective-permute-start.2 = (bf16[624,128]{1,0:T(8,128)(2,1)S(1)}, bf16[624,128]{1,0:T(8,128)(2,1)S(1)}, u32[]{:S(2)}, u32[]{:S(2)}) collective-permute-start(bf16[624,128]{1,0:T(8,128)(2,1)S(1)} %pad_maximum_fusion), channel_id=1, source_target_pairs={{4,0},{5,1},{6,2},{7,3},{0,4},{1,5},{2,6},{3,7},{12,8},{13,9},{14,... | collective-permute-start | bytes 479240 | tf_op jit(solution)/shard_map/ppermute | solution.py:287
  16.8 0.0 collective-permute-start.3
  16.8 1.0 %prepare.1 = (f32[8,128]{1,0:T(8,128)S(1)}, bf16[128,192]{1,0:T(8,128)(2,1)S(1)}, s32[128,128]{1,0:T(8,128)S(1)}, s32[128,128]{1,0:T(8,128)S(1)}) custom-call(bf16[192,128]{1,0:T(8,128)(2,1)} %bitcast.9, s32[1,128]{1,0:T(1,128)} %bitcast.10, s32[100,128]{1,0:T(8,128)} %bitcast.8, bf16[208,128]{1,0:T(8,128)(2,1)S(1)} %target.1.tgt_ref.own_ref), custom_call_target="tpu_custom_call" | custom-call | tf_op jit(solution)/shard_map/prepare/pallas_call | solution.py:311
  17.8 0.3 first_dots.1
  18.1 3.8 %collective-permute-done.3.c_ref = bf16[208,128]{1,0:T(8,128)(2,1)S(1)} collective-permute-done((bf16[208,128]{1,0:T(8,128)(2,1)S(1)}, bf16[208,128]{1,0:T(8,128)(2,1)S(1)}, u32[]{:S(2)}, u32[]{:S(2)}) %collective-permute-start.3) | collective-permute-done | bytes 53280 | tf_op jit(solution)/shard_map/ppermute | solution.py:287
  21.9 0.0 collective-permute-done.2.swap_ref
  21.9 0.4 dots.1
  22.3 1.4 %collective-permute-start.6 = (f32[112,128]{1,0:T(8,128)S(1)}, f32[112,128]{1,0:T(8,128)S(1)}, u32[]{:S(2)}, u32[]{:S(2)}) collective-permute-start(f32[112,128]{1,0:T(8,128)S(1)} %get-tuple-element.24.p0), channel_id=1, source_target_pairs={{1,0},{0,1},{3,2},{2,3},{5,4},{4,5},{7,6},{6,7},{9,8},{8,9},{11,10... | collective-permute-start | bytes 172040 | tf_op jit(solution)/shard_map/ppermute | solution.py:365
  23.7 1.9 %collective-permute-start.5 = (f32[112,128]{1,0:T(8,128)S(1)}, f32[112,128]{1,0:T(8,128)S(1)}, u32[]{:S(2)}, u32[]{:S(2)}) collective-permute-start(f32[112,128]{1,0:T(8,128)S(1)} %get-tuple-element.24.p0), channel_id=1, source_target_pairs={{3,0},{2,1},{1,2},{0,3},{7,4},{6,5},{5,6},{4,7},{11,8},{10,9},{9,1... | collective-permute-start | bytes 172040 | tf_op jit(solution)/shard_map/ppermute | solution.py:365
  25.6 0.7 %collective-permute-start.4 = (f32[112,128]{1,0:T(8,128)S(1)}, f32[112,128]{1,0:T(8,128)S(1)}, u32[]{:S(2)}, u32[]{:S(2)}) collective-permute-start(f32[112,128]{1,0:T(8,128)S(1)} %get-tuple-element.24.p0), channel_id=1, source_target_pairs={{2,0},{3,1},{0,2},{1,3},{6,4},{7,5},{4,6},{5,7},{10,8},{11,9},{8,1... | collective-permute-start | bytes 172040 | tf_op jit(solution)/shard_map/ppermute | solution.py:365
  26.3 2.8 %collective-permute-start.7 = (f32[16,128]{1,0:T(8,128)S(1)}, f32[16,128]{1,0:T(8,128)S(1)}, u32[]{:S(2)}, u32[]{:S(2)}) collective-permute-start(f32[16,128]{1,0:T(8,128)S(1)} %get-tuple-element.27), channel_id=1, source_target_pairs={{4,0},{5,1},{6,2},{7,3},{0,4},{1,5},{2,6},{3,7},{12,8},{13,9},{14,... | collective-permute-start | bytes 24584 | tf_op jit(solution)/shard_map/ppermute | solution.py:287
  29.1 0.8 %collective-permute-done.7.edge_ref = f32[16,128]{1,0:T(8,128)S(1)} collective-permute-done((f32[16,128]{1,0:T(8,128)S(1)}, f32[16,128]{1,0:T(8,128)S(1)}, u32[]{:S(2)}, u32[]{:S(2)}) %collective-permute-start.7) | collective-permute-done | bytes 8224 | tf_op jit(solution)/shard_map/ppermute | solution.py:287
  29.9 0.0 collective-permute-done.6.p3
  29.9 0.0 collective-permute-done.5.p2
  29.9 0.4 collective-permute-done.4.p1
  30.3 0.4 scores.1
  30.7 17.2 %all_to_all.5.parts_ref = f32[64,1,128]{2,1,0:T(1,128)S(1)} all-to-all(f32[64,1,128]{2,1,0:T(1,128)S(1)} %get-tuple-element.28), channel_id=1, replica_groups=mesh['frames'=64,'mp'=4] {'frames'}, dimensions={0} | all-to-all | bytes 65536 | tf_op jit(solution)/shard_map/all_to_all | solution.py:374
  47.9 0.7 %totals.1 = (f32[101,128]{1,0:T(8,128)}, f32[1,1]{1,0:T(1,128)}, f32[1,1]{1,0:T(1,128)}) custom-call(f32[64,1,128]{2,1,0:T(1,128)S(1)} %all_to_all.5.parts_ref, f32[101,128]{1,0:T(8,128)S(1)} %get-tuple-element.29.held_ref), custom_call_target="tpu_custom_call" | custom-call | tf_op jit(solution)/shard_map/totals/pallas_call | solution.py:375
  (1 shorter events, 0.0 us)
Async XLA Ops:
  2.9 10.2 %collective-permute-start.1 = (bf16[208,128]{1,0:T(8,128)(2,1)S(1)}, bf16[208,128]{1,0:T(8,128)(2,1)S(1)}, u32[]{:S(2)}, u32[]{:S(2)}) collective-permute-start(bf16[208,128]{1,0:T(8,128)(2,1)S(1)} %target.1.tgt_ref.own_ref), channel_id=1, source_target_pairs={{248,0},{249,1},{250,2},{251,3},{252,4},{253,5},{254,6},{255,7},{1... | collective-permute-start | bytes 159752 | tf_op jit(solution)/shard_map/ppermute | solution.py:287
  11.6 3.0 %collective-permute-start = (bf16[208,128]{1,0:T(8,128)(2,1)S(1)}, bf16[208,128]{1,0:T(8,128)(2,1)S(1)}, u32[]{:S(2)}, u32[]{:S(2)}) collective-permute-start(bf16[208,128]{1,0:T(8,128)(2,1)S(1)} %target.1.tgt_ref.own_ref), channel_id=1, source_target_pairs={{8,0},{9,1},{10,2},{11,3},{12,4},{13,5},{14,6},{15,7},{0,8},{1,9},... | collective-permute-start | bytes 159752 | tf_op jit(solution)/shard_map/ppermute | solution.py:287
  14.6 7.3 %collective-permute-start.2 = (bf16[624,128]{1,0:T(8,128)(2,1)S(1)}, bf16[624,128]{1,0:T(8,128)(2,1)S(1)}, u32[]{:S(2)}, u32[]{:S(2)}) collective-permute-start(bf16[624,128]{1,0:T(8,128)(2,1)S(1)} %pad_maximum_fusion), channel_id=1, source_target_pairs={{4,0},{5,1},{6,2},{7,3},{0,4},{1,5},{2,6},{3,7},{12,8},{13,9},{14,... | collective-permute-start | bytes 479240 | tf_op jit(solution)/shard_map/ppermute | solution.py:287
  16.8 5.1 %collective-permute-start.3 = (bf16[208,128]{1,0:T(8,128)(2,1)S(1)}, bf16[208,128]{1,0:T(8,128)(2,1)S(1)}, u32[]{:S(2)}, u32[]{:S(2)}) collective-permute-start(bf16[208,128]{1,0:T(8,128)(2,1)S(1)} %target.1.tgt_ref.own_ref), channel_id=1, source_target_pairs={{244,0},{245,1},{246,2},{247,3},{16,4},{17,5},{18,6},{19,7},{252,8... | collective-permute-start | bytes 159752 | tf_op jit(solution)/shard_map/ppermute | solution.py:287
  22.3 7.6 %collective-permute-start.6 = (f32[112,128]{1,0:T(8,128)S(1)}, f32[112,128]{1,0:T(8,128)S(1)}, u32[]{:S(2)}, u32[]{:S(2)}) collective-permute-start(f32[112,128]{1,0:T(8,128)S(1)} %get-tuple-element.24.p0), channel_id=1, source_target_pairs={{1,0},{0,1},{3,2},{2,3},{5,4},{4,5},{7,6},{6,7},{9,8},{8,9},{11,10... | collective-permute-start | bytes 172040 | tf_op jit(solution)/shard_map/ppermute | solution.py:365
  23.7 6.2 %collective-permute-start.5 = (f32[112,128]{1,0:T(8,128)S(1)}, f32[112,128]{1,0:T(8,128)S(1)}, u32[]{:S(2)}, u32[]{:S(2)}) collective-permute-start(f32[112,128]{1,0:T(8,128)S(1)} %get-tuple-element.24.p0), channel_id=1, source_target_pairs={{3,0},{2,1},{1,2},{0,3},{7,4},{6,5},{5,6},{4,7},{11,8},{10,9},{9,1... | collective-permute-start | bytes 172040 | tf_op jit(solution)/shard_map/ppermute | solution.py:365
  25.6 4.7 %collective-permute-start.4 = (f32[112,128]{1,0:T(8,128)S(1)}, f32[112,128]{1,0:T(8,128)S(1)}, u32[]{:S(2)}, u32[]{:S(2)}) collective-permute-start(f32[112,128]{1,0:T(8,128)S(1)} %get-tuple-element.24.p0), channel_id=1, source_target_pairs={{2,0},{3,1},{0,2},{1,3},{6,4},{7,5},{4,6},{5,7},{10,8},{11,9},{8,1... | collective-permute-start | bytes 172040 | tf_op jit(solution)/shard_map/ppermute | solution.py:365
  26.3 3.6 %collective-permute-start.7 = (f32[16,128]{1,0:T(8,128)S(1)}, f32[16,128]{1,0:T(8,128)S(1)}, u32[]{:S(2)}, u32[]{:S(2)}) collective-permute-start(f32[16,128]{1,0:T(8,128)S(1)} %get-tuple-element.27), channel_id=1, source_target_pairs={{4,0},{5,1},{6,2},{7,3},{0,4},{1,5},{2,6},{3,7},{12,8},{13,9},{14,... | collective-permute-start | bytes 24584 | tf_op jit(solution)/shard_map/ppermute | solution.py:287

commit v2 on v1

--- a/solution.py
+++ b/solution.py
@@ -213,7 +213,9 @@
 
 
 def scores_kernel(p0, p1, p2, p3, code_ref, rows_ref, probs_ref, edge_ref, scores_ref, parts_ref):
-    total = (p0[...] + p1[...]) + (p2[...] + p3[...])
+    total = (p0[...].astype(F32) + p1[...].astype(F32)) + (
+        p2[...].astype(F32) + p3[...].astype(F32)
+    )
     scale = lax.rsqrt(total[CTX_ROW : CTX_ROW + 1, :] + NORM_EPSILON) / LOGIT_SOFTNESS
     inverse = lax.rsqrt(total[OWN_NORM_ROW:, :] + NORM_EPSILON)
     own = total[SELF_ROW : SELF_ROW + 1, :] * inverse[0:1, :] * scale
@@ -360,9 +362,10 @@
         name="dots",
     )(picked, norms, probs, swap, c, ctx, code_tk, rows)
     edge = send(edge, source=lambda s: s ^ 1)
+    narrow = payload.astype(BF16)
     peers = []
     for step in (2, 3, 1):
-        peers.append(lax.ppermute(payload, "mp", [(j ^ step, j) for j in range(replicas)]))
+        peers.append(lax.ppermute(narrow, "mp", [(j ^ step, j) for j in range(replicas)]))
     scores_t, parts = pl.pallas_call(
         scores_kernel,
         out_shape=(struct((NEG + 1, count), F32), struct((shards, 1, 128), F32)),
@@ -370,7 +373,7 @@
         out_specs=[pl.BlockSpec(memory_space=VMEM)] * 2,
         compiler_params=PARAMS,
         name="scores",
-    )(payload, *peers, code_kt, rows, probs, edge)
+    )(narrow, *peers, code_kt, rows, probs, edge)
     parts = lax.all_to_all(parts, "frames", split_axis=0, concat_axis=0, tiled=True)
     scores_t, loss, diversity = pl.pallas_call(
         functools.partial(totals_kernel, count * shards),

time: 48.8 us -> 48.5 us (level)
  transfers between devices with their start and end apart: 8 -> 8, of which waited for: 5 -> 4; matrix products, arithmetic and copies ran while one was open for 0% -> 0% of each run, Pallas kernels for 3% -> 3%
where the time goes in v2:
time: 48.5 us; the launch traced here: 48.3 us
  starting transfers between devices  17.7 us (36%)
  blocking collectives  17.3 us (36%)
  waiting for transfers between devices  7.57 us (16%)
  Pallas kernels  5.07 us (10%)
  between operations  0.68 us (1%)
    all_to_all x1, blocking collectives, on_device(): lax.all_to_all(parts, 'frames', split_axis=0, concat_axis=0, tiled=True)  17.3 us
    ppermute x5, starting transfers between devices, exchange(): return lax.ppermute(value, ('frames', 'mp'), pairs)  13.6 us
    ppermute x5, waiting for transfers between devices, exchange(): return lax.ppermute(value, ('frames', 'mp'), pairs)  7.56 us
    ppermute x3, starting transfers between devices, on_device(): lax.ppermute(narrow, 'mp', [(j ^ step, j) for j in range(replicas)])  4.01 us
    pallas_call x1, Pallas kernels, on_device(): pl.pallas_call(target_kernel, out_shape=struct((width + PROB_ROWS, count)...  2.29 us
    pallas_call x1, Pallas kernels, on_device(): pl.pallas_call(prepare_kernel, out_shape=(struct((8, count), F32), struct...  1.01 us
  transfers between devices with their start and end apart: 8, of which 4 were waited for; matrix products, arithmetic and copies ran while one was open for 0% of the time, Pallas kernels for 3%

profile of v2, /device:TPU:1, one launch (start us, length us, event | category | flops | bytes accessed | tf_op | source)
XLA Modules:
  0.0 48.3 jit_solution(5177686197358242921)
XLA Ops:
  0.6 2.3 %target.1.tgt_ref.own_ref = bf16[208,128]{1,0:T(8,128)(2,1)S(1)} custom-call(bf16[128,512]{1,0:T(8,128)(2,1)} %feat_hbm.1, bf16[512,640]{1,0:T(8,128)(2,1)} %lw_hbm.1, f32[128,640]{1,0:T(8,128)} %gum_hbm.1, bf16[640,384]{1,0:T(8,128)(2,1)} %cb_hbm.1, bf16[192,768]{1,0:T(8,128)(2,1)} %bitcast.7), custom_call_target="tpu_custom_call" | custom-call | tf_op jit(solution)/shard_map/target/pallas_call | solution.py:302
  2.9 8.7 %collective-permute-start.1 = (bf16[208,128]{1,0:T(8,128)(2,1)S(1)}, bf16[208,128]{1,0:T(8,128)(2,1)S(1)}, u32[]{:S(2)}, u32[]{:S(2)}) collective-permute-start(bf16[208,128]{1,0:T(8,128)(2,1)S(1)} %target.1.tgt_ref.own_ref), channel_id=1, source_target_pairs={{248,0},{249,1},{250,2},{251,3},{252,4},{253,5},{254,6},{255,7},{1... | collective-permute-start | bytes 159752 | tf_op jit(solution)/shard_map/ppermute | solution.py:289
  11.6 0.0 collective-permute-start
  11.6 1.5 %collective-permute-done.1.b_ref = bf16[208,128]{1,0:T(8,128)(2,1)S(1)} collective-permute-done((bf16[208,128]{1,0:T(8,128)(2,1)S(1)}, bf16[208,128]{1,0:T(8,128)(2,1)S(1)}, u32[]{:S(2)}, u32[]{:S(2)}) %collective-permute-start.1) | collective-permute-done | bytes 53280 | tf_op jit(solution)/shard_map/ppermute | solution.py:289
  13.1 1.5 %collective-permute-done.a_ref = bf16[208,128]{1,0:T(8,128)(2,1)S(1)} collective-permute-done((bf16[208,128]{1,0:T(8,128)(2,1)S(1)}, bf16[208,128]{1,0:T(8,128)(2,1)S(1)}, u32[]{:S(2)}, u32[]{:S(2)}) %collective-permute-start) | collective-permute-done | bytes 53280 | tf_op jit(solution)/shard_map/ppermute | solution.py:289
  14.6 2.2 %collective-permute-start.2 = (bf16[624,128]{1,0:T(8,128)(2,1)S(1)}, bf16[624,128]{1,0:T(8,128)(2,1)S(1)}, u32[]{:S(2)}, u32[]{:S(2)}) collective-permute-start(bf16[624,128]{1,0:T(8,128)(2,1)S(1)} %pad_maximum_fusion), channel_id=1, source_target_pairs={{4,0},{5,1},{6,2},{7,3},{0,4},{1,5},{2,6},{3,7},{12,8},{13,9},{14,... | collective-permute-start | bytes 479240 | tf_op jit(solution)/shard_map/ppermute | solution.py:289
  16.8 0.0 collective-permute-start.3
  16.8 1.0 %prepare.1 = (f32[8,128]{1,0:T(8,128)S(1)}, bf16[128,192]{1,0:T(8,128)(2,1)S(1)}, s32[128,128]{1,0:T(8,128)S(1)}, s32[128,128]{1,0:T(8,128)S(1)}) custom-call(bf16[192,128]{1,0:T(8,128)(2,1)} %bitcast.9, s32[1,128]{1,0:T(1,128)} %bitcast.10, s32[100,128]{1,0:T(8,128)} %bitcast.8, bf16[208,128]{1,0:T(8,128)(2,1)S(1)} %target.1.tgt_ref.own_ref), custom_call_target="tpu_custom_call" | custom-call | tf_op jit(solution)/shard_map/prepare/pallas_call | solution.py:313
  17.8 0.3 first_dots.1
  18.1 3.8 %collective-permute-done.3.c_ref = bf16[208,128]{1,0:T(8,128)(2,1)S(1)} collective-permute-done((bf16[208,128]{1,0:T(8,128)(2,1)S(1)}, bf16[208,128]{1,0:T(8,128)(2,1)S(1)}, u32[]{:S(2)}, u32[]{:S(2)}) %collective-permute-start.3) | collective-permute-done | bytes 53280 | tf_op jit(solution)/shard_map/ppermute | solution.py:289
  21.9 0.0 collective-permute-done.2.swap_ref
  21.9 0.4 dots.1
  22.3 1.4 %collective-permute-start.6 = (bf16[112,128]{1,0:T(8,128)(2,1)S(1)}, bf16[112,128]{1,0:T(8,128)(2,1)S(1)}, u32[]{:S(2)}, u32[]{:S(2)}) collective-permute-start(bf16[112,128]{1,0:T(8,128)(2,1)S(1)} %convert_element_type.3.p0), channel_id=1, source_target_pairs={{1,0},{0,1},{3,2},{2,3},{5,4},{4,5},{7,6},{6,7},{9,8},{8,9},{11,10... | collective-permute-start | bytes 86024 | tf_op jit(solution)/shard_map/ppermute | solution.py:368
  23.7 1.9 %collective-permute-start.5 = (bf16[112,128]{1,0:T(8,128)(2,1)S(1)}, bf16[112,128]{1,0:T(8,128)(2,1)S(1)}, u32[]{:S(2)}, u32[]{:S(2)}) collective-permute-start(bf16[112,128]{1,0:T(8,128)(2,1)S(1)} %convert_element_type.3.p0), channel_id=1, source_target_pairs={{3,0},{2,1},{1,2},{0,3},{7,4},{6,5},{5,6},{4,7},{11,8},{10,9},{9,1... | collective-permute-start | bytes 86024 | tf_op jit(solution)/shard_map/ppermute | solution.py:368
  25.6 0.7 %collective-permute-start.4 = (bf16[112,128]{1,0:T(8,128)(2,1)S(1)}, bf16[112,128]{1,0:T(8,128)(2,1)S(1)}, u32[]{:S(2)}, u32[]{:S(2)}) collective-permute-start(bf16[112,128]{1,0:T(8,128)(2,1)S(1)} %convert_element_type.3.p0), channel_id=1, source_target_pairs={{2,0},{3,1},{0,2},{1,3},{6,4},{7,5},{4,6},{5,7},{10,8},{11,9},{8,1... | collective-permute-start | bytes 86024 | tf_op jit(solution)/shard_map/ppermute | solution.py:368
  26.3 2.8 %collective-permute-start.7 = (f32[16,128]{1,0:T(8,128)S(1)}, f32[16,128]{1,0:T(8,128)S(1)}, u32[]{:S(2)}, u32[]{:S(2)}) collective-permute-start(f32[16,128]{1,0:T(8,128)S(1)} %get-tuple-element.27), channel_id=1, source_target_pairs={{4,0},{5,1},{6,2},{7,3},{0,4},{1,5},{2,6},{3,7},{12,8},{13,9},{14,... | collective-permute-start | bytes 24584 | tf_op jit(solution)/shard_map/ppermute | solution.py:289
  29.1 0.8 %collective-permute-done.7.edge_ref = f32[16,128]{1,0:T(8,128)S(1)} collective-permute-done((f32[16,128]{1,0:T(8,128)S(1)}, f32[16,128]{1,0:T(8,128)S(1)}, u32[]{:S(2)}, u32[]{:S(2)}) %collective-permute-start.7) | collective-permute-done | bytes 8224 | tf_op jit(solution)/shard_map/ppermute | solution.py:289
  29.9 0.0 collective-permute-done.6.p3
  29.9 0.0 collective-permute-done.5.p2
  29.9 0.0 collective-permute-done.4.p1
  29.9 0.4 scores.1
  30.3 17.3 %all_to_all.5.parts_ref = f32[64,1,128]{2,1,0:T(1,128)S(1)} all-to-all(f32[64,1,128]{2,1,0:T(1,128)S(1)} %get-tuple-element.28), channel_id=1, replica_groups=mesh['frames'=64,'mp'=4] {'frames'}, dimensions={0} | all-to-all | bytes 65536 | tf_op jit(solution)/shard_map/all_to_all | solution.py:377
  47.6 0.7 %totals.1 = (f32[101,128]{1,0:T(8,128)}, f32[1,1]{1,0:T(1,128)}, f32[1,1]{1,0:T(1,128)}) custom-call(f32[64,1,128]{2,1,0:T(1,128)S(1)} %all_to_all.5.parts_ref, f32[101,128]{1,0:T(8,128)S(1)} %get-tuple-element.29.held_ref), custom_call_target="tpu_custom_call" | custom-call | tf_op jit(solution)/shard_map/totals/pallas_call | solution.py:378
  (2 shorter events, 0.0 us)
Async XLA Ops:
  2.9 10.2 %collective-permute-start.1 = (bf16[208,128]{1,0:T(8,128)(2,1)S(1)}, bf16[208,128]{1,0:T(8,128)(2,1)S(1)}, u32[]{:S(2)}, u32[]{:S(2)}) collective-permute-start(bf16[208,128]{1,0:T(8,128)(2,1)S(1)} %target.1.tgt_ref.own_ref), channel_id=1, source_target_pairs={{248,0},{249,1},{250,2},{251,3},{252,4},{253,5},{254,6},{255,7},{1... | collective-permute-start | bytes 159752 | tf_op jit(solution)/shard_map/ppermute | solution.py:289
  11.6 3.0 %collective-permute-start = (bf16[208,128]{1,0:T(8,128)(2,1)S(1)}, bf16[208,128]{1,0:T(8,128)(2,1)S(1)}, u32[]{:S(2)}, u32[]{:S(2)}) collective-permute-start(bf16[208,128]{1,0:T(8,128)(2,1)S(1)} %target.1.tgt_ref.own_ref), channel_id=1, source_target_pairs={{8,0},{9,1},{10,2},{11,3},{12,4},{13,5},{14,6},{15,7},{0,8},{1,9},... | collective-permute-start | bytes 159752 | tf_op jit(solution)/shard_map/ppermute | solution.py:289
  14.6 7.3 %collective-permute-start.2 = (bf16[624,128]{1,0:T(8,128)(2,1)S(1)}, bf16[624,128]{1,0:T(8,128)(2,1)S(1)}, u32[]{:S(2)}, u32[]{:S(2)}) collective-permute-start(bf16[624,128]{1,0:T(8,128)(2,1)S(1)} %pad_maximum_fusion), channel_id=1, source_target_pairs={{4,0},{5,1},{6,2},{7,3},{0,4},{1,5},{2,6},{3,7},{12,8},{13,9},{14,... | collective-permute-start | bytes 479240 | tf_op jit(solution)/shard_map/ppermute | solution.py:289
  16.8 5.1 %collective-permute-start.3 = (bf16[208,128]{1,0:T(8,128)(2,1)S(1)}, bf16[208,128]{1,0:T(8,128)(2,1)S(1)}, u32[]{:S(2)}, u32[]{:S(2)}) collective-permute-start(bf16[208,128]{1,0:T(8,128)(2,1)S(1)} %target.1.tgt_ref.own_ref), channel_id=1, source_target_pairs={{244,0},{245,1},{246,2},{247,3},{16,4},{17,5},{18,6},{19,7},{252,8... | collective-permute-start | bytes 159752 | tf_op jit(solution)/shard_map/ppermute | solution.py:289
  22.3 7.6 %collective-permute-start.6 = (bf16[112,128]{1,0:T(8,128)(2,1)S(1)}, bf16[112,128]{1,0:T(8,128)(2,1)S(1)}, u32[]{:S(2)}, u32[]{:S(2)}) collective-permute-start(bf16[112,128]{1,0:T(8,128)(2,1)S(1)} %convert_element_type.3.p0), channel_id=1, source_target_pairs={{1,0},{0,1},{3,2},{2,3},{5,4},{4,5},{7,6},{6,7},{9,8},{8,9},{11,10... | collective-permute-start | bytes 86024 | tf_op jit(solution)/shard_map/ppermute | solution.py:368
  23.7 6.2 %collective-permute-start.5 = (bf16[112,128]{1,0:T(8,128)(2,1)S(1)}, bf16[112,128]{1,0:T(8,128)(2,1)S(1)}, u32[]{:S(2)}, u32[]{:S(2)}) collective-permute-start(bf16[112,128]{1,0:T(8,128)(2,1)S(1)} %convert_element_type.3.p0), channel_id=1, source_target_pairs={{3,0},{2,1},{1,2},{0,3},{7,4},{6,5},{5,6},{4,7},{11,8},{10,9},{9,1... | collective-permute-start | bytes 86024 | tf_op jit(solution)/shard_map/ppermute | solution.py:368
  25.6 4.3 %collective-permute-start.4 = (bf16[112,128]{1,0:T(8,128)(2,1)S(1)}, bf16[112,128]{1,0:T(8,128)(2,1)S(1)}, u32[]{:S(2)}, u32[]{:S(2)}) collective-permute-start(bf16[112,128]{1,0:T(8,128)(2,1)S(1)} %convert_element_type.3.p0), channel_id=1, source_target_pairs={{2,0},{3,1},{0,2},{1,3},{6,4},{7,5},{4,6},{5,7},{10,8},{11,9},{8,1... | collective-permute-start | bytes 86024 | tf_op jit(solution)/shard_map/ppermute | solution.py:368
  26.3 3.6 %collective-permute-start.7 = (f32[16,128]{1,0:T(8,128)S(1)}, f32[16,128]{1,0:T(8,128)S(1)}, u32[]{:S(2)}, u32[]{:S(2)}) collective-permute-start(f32[16,128]{1,0:T(8,128)S(1)} %get-tuple-element.27), channel_id=1, source_target_pairs={{4,0},{5,1},{6,2},{7,3},{0,4},{1,5},{2,6},{3,7},{12,8},{13,9},{14,... | collective-permute-start | bytes 24584 | tf_op jit(solution)/shard_map/ppermute | solution.py:289
